TPU v7x, 32 devices: a whole 2x2x4 slice. The times are simulated.
32 devices in a mesh: groups: 2 (over x), az: 16 (over z, y, core).
Axes of the slice: x: 2, y: 2, z: 4, core: 2. Of those that a mesh axis runs over, the one named last changes fastest.
Arguments:
- sweep_stack: bfloat16 [2, 4, 32, 80, 2560], P(None, None, ('groups', 'az')), parts along dimension 2
- blend_curve: bfloat16 [32, 80], P(('groups', 'az')), parts along dimension 0, may hold values from 0.25 to 4
- sweep_start_index: int32 [32], P(('groups', 'az')), parts along dimension 0, may hold values from -20 to 610, as said below
- usable_azimuth_extent: int32 [32, 2], P(('groups', 'az')), parts along dimension 0, may hold values from 0 to 80, as said below
- usable_column_extent: int32 [32, 2], P(('groups', 'az')), parts along dimension 0, may hold values from 0 to 2560, as said below
- image_couples: int32 [8, 2], P('groups'), parts along dimension 0, may hold values from 0 to 3, as said below
Outputs:
- interferogram: float32 [2, 8, 128, 128], P(None, 'groups', 'az'), parts along dimension 1
- coherence: float32 [8, 128, 128], P('groups', 'az'), parts along dimension 0
There are 2 independent parts, one for each index of `groups`. A program takes and returns all parts, laid end to end along the dimension named above; each array names one. Nothing has to cross between parts.
Inputs may be any that keep to these rules, and one draw needn't show every extreme that they name: `sweep_start_index`: the valid lines of burst b lie at merged rows from b * 40 - 15 to (b + 1) * 40 + 14, and some burst reaches both ends. The valid lines of all bursts together cover every merged row from 0 to 639. `usable_azimuth_extent`: first below end for every burst. `usable_column_extent`: first below end for every burst. `image_couples`: the two acquisitions of a pair differ.
All inputs are finite; a program needn't handle non-finite values.
Results may differ from a plain program's by a relative error of at most 0.0003.
Values may be sent and summed in bfloat16 or wider, within the bound.
A program may use at most 64 MiB of HBM per device.

v0:
```python
import jax
import jax.numpy as jnp
from jax import lax
from jax.sharding import PartitionSpec as P

BLOCK_HEIGHT = 40
SLANT_WIDTH = 2560
LOOK_ROWS = 5
LOOK_COLS = 20
MARGIN = 15
SWEEP_HEIGHT = 80


def from_behind(block, axis, distance):
    devices = range(lax.axis_size(axis))
    route = [(i - distance, i) for i in devices if i - distance in devices]
    return lax.ppermute(block, axis, route)


def looked(values, column_box):
    shaped = values.reshape(
        values.shape[:-2] + (values.shape[-2] // LOOK_ROWS, LOOK_ROWS, values.shape[-1])
    )
    aggregate = jnp.sum(shaped, axis=-2)
    return jnp.dot(aggregate, column_box, precision=lax.Precision.HIGHEST)


def weighted(raw_lines, weights):
    return raw_lines.astype(jnp.float32) * weights.astype(jnp.float32)[:, None]


def per_device(
    sweep_stack,
    blend_curve,
    sweep_start_index,
    usable_azimuth_extent,
    usable_column_extent,
    image_couples,
):
    sweep_content = sweep_stack[:, :, 0]
    block_height = BLOCK_HEIGHT
    azimuth_index = jnp.arange(SWEEP_HEIGHT, dtype=jnp.int32)
    column_index = jnp.arange(SLANT_WIDTH, dtype=jnp.int32)
    line_valid = (azimuth_index >= usable_azimuth_extent[0, 0]) & (
        azimuth_index < usable_azimuth_extent[0, 1]
    )
    azimuth_blend = jnp.where(line_valid, blend_curve[0], jnp.zeros((), jnp.bfloat16))
    sample_valid = (column_index >= usable_column_extent[0, 0]) & (
        column_index < usable_column_extent[0, 1]
    )
    index_shift = sweep_start_index[0] - (lax.axis_index("az") - 1) * block_height

    def gather_lines(start_index, count):
        desired = start_index + jnp.arange(count, dtype=jnp.int32) - index_shift
        within_extent = (desired >= 0) & (desired < SWEEP_HEIGHT)
        bounded_indices = jnp.clip(desired, 0, SWEEP_HEIGHT - 1)
        chosen_indices = jnp.take(sweep_content, bounded_indices, axis=2)
        raw_lines = jnp.where(sample_valid, chosen_indices, jnp.zeros((), jnp.bfloat16))
        matches = bounded_indices[:, None] == azimuth_index[None, :]
        weights = jnp.sum(
            jnp.where(matches, azimuth_blend[None, :], jnp.zeros((), jnp.bfloat16)), axis=1
        )
        weights = jnp.where(within_extent, weights, jnp.zeros((), jnp.bfloat16))
        return (raw_lines, weights)

    extent_rows = MARGIN
    middle_lines, middle_weights = gather_lines(block_height, block_height)
    lower_lines, lower_weights = gather_lines(block_height - extent_rows, extent_rows)
    upper_lines, upper_weights = gather_lines(2 * block_height, extent_rows)
    from_above, above_weights = from_behind(
        (weighted(lower_lines, lower_weights), lower_weights.astype(jnp.float32)), "az", -1
    )
    from_below, below_weights = from_behind(
        (weighted(upper_lines, upper_weights), upper_weights.astype(jnp.float32)), "az", 1
    )
    cross_term = weighted(middle_lines, middle_weights)
    cross_term = cross_term.at[:, :, block_height - extent_rows :].add(from_above)
    cross_term = cross_term.at[:, :, :extent_rows].add(from_below)
    intensity_norm = middle_weights.astype(jnp.float32)
    intensity_norm = intensity_norm.at[block_height - extent_rows :].add(above_weights)
    intensity_norm = intensity_norm.at[:extent_rows].add(below_weights)
    combined_grid = cross_term / intensity_norm[:, None]
    intensity = combined_grid[0] * combined_grid[0] + combined_grid[1] * combined_grid[1]
    first_image = jnp.take(combined_grid, image_couples[:, 0], axis=1)
    second_image = jnp.take(combined_grid, image_couples[:, 1], axis=1)
    real_part = first_image[0] * second_image[0] + first_image[1] * second_image[1]
    imag_part = first_image[1] * second_image[0] - first_image[0] * second_image[1]
    column_box = (
        column_index[:, None] // LOOK_COLS
        == jnp.arange(SLANT_WIDTH // LOOK_COLS, dtype=jnp.int32)[None, :]
    ).astype(jnp.float32)
    look_sum = looked(jnp.stack([real_part, imag_part]), column_box)
    look_power = looked(intensity, column_box)
    power_first = jnp.take(look_power, image_couples[:, 0], axis=0)
    power_second = jnp.take(look_power, image_couples[:, 1], axis=0)
    coherence = (look_sum[0] * look_sum[0] + look_sum[1] * look_sum[1]) / jnp.maximum(
        power_first * power_second, 1.0
    )
    interferogram = look_sum / (LOOK_ROWS * LOOK_COLS)
    return (interferogram, coherence)


def solution(mesh):
    return jax.shard_map(
        per_device,
        mesh=mesh,
        in_specs=(
            P(None, None, ("groups", "az"), None, None),
            P(("groups", "az"), None),
            P(("groups", "az")),
            P(("groups", "az"), None),
            P(("groups", "az"), None),
            P("groups", None),
        ),
        out_specs=(P(None, "groups", "az", None), P("groups", "az", None)),
        check_vma=False,
    )
```

profile of v0, /device:TPU:11, one launch (start us, length us, event | category | flops | bytes accessed | tf_op | source)
XLA Modules:
  0.0 83.5 jit_solution(15054228062552306891)
XLA Ops:
  1.3 1.4 %fusion.35 = (s32[1,1]{1,0:T(1,128)}, s32[1,1]{1,0:T(1,128)}) fusion(s32[1,2]{1,0:T(1,128)} %param.23), kind=kLoop, calls=%fused_computation.96 | loop fusion | bytes 16 | tf_op jit(solution)/shard_map/slice | solution.py:44
  2.7 1.9 %fusion.27 = bf16[80]{0:T(256)(128)(2,1)S(1)} fusion(bf16[1,80]{1,0:T(2,128)(2,1)} %param.21, s32[]{:T(128)} %bitcast.7, s32[]{:T(128)} %bitcast.6), kind=kLoop, calls=%fused_computation.87 | loop fusion | flops 320 | bytes 328 | tf_op jit(solution)/shard_map/jit(_where)/broadcast_in_dim | solution.py:61
  4.8 2.6 %collective-permute-start.2 = (f32[15]{0:T(128)S(1)}, f32[15]{0:T(128)S(1)}, u32[]{:S(2)}, u32[]{:S(2)}) collective-permute-start(f32[15]{0:T(128)S(1)} %fusion.29), channel_id=1, source_target_pairs={{1,0},{2,1},{3,2},{4,3},{5,4},{6,5},{7,6},{8,7},{9,8},{10,9},{11,1... | collective-permute-start | bytes 188 | tf_op jit(solution)/shard_map/ppermute | solution.py:17
  7.4 3.0 %collective-permute-start.3 = (f32[15]{0:T(128)S(1)}, f32[15]{0:T(128)S(1)}, u32[]{:S(2)}, u32[]{:S(2)}) collective-permute-start(f32[15]{0:T(128)S(1)} %fusion.30), channel_id=1, source_target_pairs={{0,1},{1,2},{2,3},{3,4},{4,5},{5,6},{6,7},{7,8},{8,9},{9,10},{10,1... | collective-permute-start | bytes 188 | tf_op jit(solution)/shard_map/ppermute | solution.py:17
  10.5 1.3 %fusion.34 = (s32[1,1]{1,0:T(1,128)}, s32[1,1]{1,0:T(1,128)}) fusion(s32[1,2]{1,0:T(1,128)} %param.24), kind=kLoop, calls=%fused_computation.95 | loop fusion | bytes 16 | tf_op jit(solution)/shard_map/slice | solution.py:48
  11.8 4.5 %copy.51 = bf16[2,4,1,80,2560]{4,1,3,0,2:T(4,128)(2,1)S(1)} copy(bf16[2,4,1,80,2560]{4,3,2,1,0:T(8,128)(2,1)} %param.20) | data formatting | bytes 6553600 | tf_op args[0]
  16.3 1.9 %gather_fusion.2 = bf16[15,2,4,2560]{3,2,1,0:T(4,128)(2,1)} fusion(bf16[2,4,80,2560]{3,1,2,0:T(4,128)(2,1)S(1)} %bitcast.52, s32[1024]{0:T(1024)S(1)} %pad_clamp_fusion.2), kind=kCustom, calls=%fused_computation.3.clone | custom fusion | bytes 1228860 | tf_op jit(solution)/shard_map/jit(_take)/gather | solution.py:57
  18.1 1.9 %gather_fusion.1 = bf16[15,2,4,2560]{3,2,1,0:T(4,128)(2,1)} fusion(bf16[2,4,80,2560]{3,1,2,0:T(4,128)(2,1)S(1)} %bitcast.53, s32[1024]{0:T(1024)S(1)} %pad_clamp_fusion.3), kind=kCustom, calls=%fused_computation.clone | custom fusion | bytes 1228860 | tf_op jit(solution)/shard_map/jit(_take)/gather | solution.py:57
  20.0 1.3 %fusion.19 = pred[2560]{0:T(1024)(128)(4,1)S(1)} fusion(s32[]{:T(128)} %bitcast.2, s32[]{:T(128)} %bitcast.1), kind=kLoop, calls=%fused_computation.53 | loop fusion | flops 7680 | bytes 2568 | tf_op jit(solution)/shard_map/and | solution.py:48
  21.4 3.6 %convert_multiply_fusion = (f32[2,4,15,2560]{3,1,0,2:T(4,128)}, f32[2,4,15,2560]{3,1,0,2:T(4,128)}) fusion(bf16[15,2,4,2560]{3,2,1,0:T(4,128)(2,1)} %gather_fusion.2, f32[15]{0:T(128)S(1)} %fusion.30, pred[15]{0:T(512)(128)(4,1)S(1)} %get-tuple-element.77, pred[2560]{0:T(1024)(128)(4,1)S(1)} %fusion.19, f32[15]{0:T(128)S(1)} %fusion.29, ...), kind=kLoop, calls=%fused_computation.27 | loop fusion | flops 2457600 | bytes 3689110 | tf_op jit(solution)/shard_map/mul | solution.py:29
  25.0 2.4 %collective-permute-start.1 = (f32[2,4,15,2560]{3,1,0,2:T(4,128)}, f32[2,4,15,2560]{3,1,0,2:T(4,128)}, u32[]{:S(2)}, u32[]{:S(2)}) collective-permute-start(f32[2,4,15,2560]{3,1,0,2:T(4,128)} %get-tuple-element.65), channel_id=1, source_target_pairs={{0,1},{1,2},{2,3},{3,4},{4,5},{5,6},{6,7},{7,8},{8,9},{9,10},{10,1... | collective-permute-start | bytes 3686408 | tf_op jit(solution)/shard_map/ppermute | solution.py:17
  27.4 2.1 %collective-permute-start = (f32[2,4,15,2560]{3,1,0,2:T(4,128)}, f32[2,4,15,2560]{3,1,0,2:T(4,128)}, u32[]{:S(2)}, u32[]{:S(2)}) collective-permute-start(f32[2,4,15,2560]{3,1,0,2:T(4,128)} %get-tuple-element.66), channel_id=1, source_target_pairs={{1,0},{2,1},{3,2},{4,3},{5,4},{6,5},{7,6},{8,7},{9,8},{10,9},{11,1... | collective-permute-start | bytes 3686408 | tf_op jit(solution)/shard_map/ppermute | solution.py:17
  29.8 3.4 %gather_fusion = bf16[40,2,4,2560]{3,2,1,0:T(4,128)(2,1)} fusion(bf16[2,4,80,2560]{3,1,2,0:T(4,128)(2,1)S(1)} %bitcast.54, s32[1024]{0:T(1024)S(1)} %pad_clamp_fusion.4), kind=kCustom, calls=%fused_computation.6 | custom fusion | bytes 3276960 | tf_op jit(solution)/shard_map/jit(_take)/gather | solution.py:57
  33.2 2.6 %multiply_bitcast_fusion = f32[2,4,40,2560]{3,1,0,2:T(4,128)S(1)} fusion(f32[40]{0:T(128)S(1)} %fusion.28, bf16[40,2,4,2560]{3,2,1,0:T(4,128)(2,1)} %gather_fusion, pred[40]{0:T(512)(128)(4,1)S(1)} %compare_and_fusion.4, pred[2560]{0:T(1024)(128)(4,1)S(1)} %fusion.19), kind=kLoop, calls=%fused_computation.11 | loop fusion | flops 3276800 | bytes 4917960 | tf_op jit(solution)/shard_map/mul | solution.py:29
  36.0 20.5 %collective-permute-done = f32[2,4,15,2560]{3,1,0,2:T(4,128)} collective-permute-done((f32[2,4,15,2560]{3,1,0,2:T(4,128)}, f32[2,4,15,2560]{3,1,0,2:T(4,128)}, u32[]{:S(2)}, u32[]{:S(2)}) %collective-permute-start) | collective-permute-done | bytes 1228832 | tf_op jit(solution)/shard_map/ppermute | solution.py:17
  56.4 1.7 %fusion.8 = f32[2,4,40,2560]{3,1,0,2:T(4,128)S(1)} fusion(f32[2,4,40,2560]{3,1,0,2:T(4,128)S(1)} %multiply_bitcast_fusion, f32[2,4,15,2560]{3,1,0,2:T(4,128)} %collective-permute-done), kind=kLoop, calls=%fused_computation.26 | loop fusion | flops 307200 | bytes 3686400 | tf_op jit(solution)/shard_map/scatter-add | solution.py:77
  58.1 1.7 %fusion.7 = f32[2,4,40,2560]{3,1,0,2:T(4,128)S(1)} fusion(f32[2,4,40,2560]{3,1,0,2:T(4,128)S(1)} %fusion.8, f32[2,4,15,2560]{3,1,0,2:T(4,128)} %collective-permute-done.1), kind=kLoop, calls=%fused_computation.24 | loop fusion | flops 307200 | bytes 3686400 | tf_op jit(solution)/shard_map/scatter-add | solution.py:78
  60.7 1.6 %fusion = f32[1,4,40,2560]{3,1,0,2:T(4,128)} fusion(f32[2,4,40,2560]{3,1,0,2:T(4,128)S(1)} %broadcast_divide_fusion), kind=kLoop, calls=%fused_computation.13 | loop fusion | flops 1228800 | bytes 4915200 | tf_op jit(solution)/shard_map/add | solution.py:83
  62.3 1.9 %copy.29 = f32[2,4,40,2560]{3,2,1,0:T(8,128)S(1)} copy(f32[2,4,40,2560]{3,1,0,2:T(4,128)S(1)} %broadcast_divide_fusion) | data formatting | bytes 6553600 | tf_op jit(solution)/shard_map/div | solution.py:82
  64.2 2.5 %reduce_sum.58 = f32[4,8,2560]{2,0,1:T(4,128)} reduce(f32[4,8,5,2560]{3,0,2,1:T(4,128)} %bitcast.56, f32[]{:T(128)} %constant.178.clone.1), dimensions={2}, to_apply=%region_4.7 | reduce | flops 327680 | bytes 1966084 | tf_op jit(solution)/shard_map/reduce_sum | solution.py:24
  66.7 1.8 %fusion.5 = f32[4,8,128]{2,0,1:T(4,128)S(1)} fusion(f32[4,8,2560]{2,0,1:T(4,128)} %reduce_sum.58, s32[2560]{0:T(1024)S(1)} %add_select_fusion), kind=kOutput, calls=%fused_computation.22 | convolution fusion | flops 126156800 | bytes 354304 | tf_op jit(solution)/shard_map/dot_general | solution.py:25
  69.6 2.4 %gather_fusion.3 = f32[4,2,40,2560]{3,2,1,0:T(8,128)} fusion(f32[2,4,40,2560]{3,2,1,0:T(8,128)S(1)} %copy.29, s32[1024]{0:T(1024)S(1)} %get-tuple-element.82), kind=kCustom, calls=%fused_computation.1.clone | custom fusion | bytes 6553616 | tf_op jit(solution)/shard_map/jit(_take)/gather | solution.py:84
  72.0 2.5 %gather_fusion.4 = f32[4,2,40,2560]{3,2,1,0:T(8,128)} fusion(f32[2,4,40,2560]{3,2,1,0:T(8,128)S(1)} %copy.29, s32[1024]{0:T(1024)S(1)} %get-tuple-element.81), kind=kCustom, calls=%fused_computation.4.clone | custom fusion | bytes 6553616 | tf_op jit(solution)/shard_map/jit(_take)/gather | solution.py:85
  74.5 2.5 %select_bitcast_fusion = f32[2,4,40,2560]{3,2,0,1:T(8,128)S(1)} fusion(f32[4,2,40,2560]{3,2,1,0:T(8,128)} %gather_fusion.4, pred[4]{0:T(512)(128)(4,1)S(1)} %get-tuple-element.67), kind=kLoop, calls=%fused_computation.9 | loop fusion | flops 819200 | bytes 6553604 | tf_op jit(solution)/shard_map/jit(_take)/select_n | solution.py:85
  (39 shorter events, 9.1 us)
Async XLA Ops:
  4.8 31.0 %collective-permute-start.2 = (f32[15]{0:T(128)S(1)}, f32[15]{0:T(128)S(1)}, u32[]{:S(2)}, u32[]{:S(2)}) collective-permute-start(f32[15]{0:T(128)S(1)} %fusion.29), channel_id=1, source_target_pairs={{1,0},{2,1},{3,2},{4,3},{5,4},{6,5},{7,6},{8,7},{9,8},{10,9},{11,1... | collective-permute-start | bytes 188 | tf_op jit(solution)/shard_map/ppermute | solution.py:17
  7.4 28.5 %collective-permute-start.3 = (f32[15]{0:T(128)S(1)}, f32[15]{0:T(128)S(1)}, u32[]{:S(2)}, u32[]{:S(2)}) collective-permute-start(f32[15]{0:T(128)S(1)} %fusion.30), channel_id=1, source_target_pairs={{0,1},{1,2},{2,3},{3,4},{4,5},{5,6},{6,7},{7,8},{8,9},{9,10},{10,1... | collective-permute-start | bytes 188 | tf_op jit(solution)/shard_map/ppermute | solution.py:17
  21.4 8.4 %copy-start.1 = (s32[4,2]{0,1:T(2,128)S(1)}, s32[4,2]{0,1:T(2,128)}, u32[]{:S(2)}) copy-start(s32[4,2]{0,1:T(2,128)} %param.25) | copy-start | bytes 100
  25.0 33.1 %collective-permute-start.1 = (f32[2,4,15,2560]{3,1,0,2:T(4,128)}, f32[2,4,15,2560]{3,1,0,2:T(4,128)}, u32[]{:S(2)}, u32[]{:S(2)}) collective-permute-start(f32[2,4,15,2560]{3,1,0,2:T(4,128)} %get-tuple-element.65), channel_id=1, source_target_pairs={{0,1},{1,2},{2,3},{3,4},{4,5},{5,6},{6,7},{7,8},{8,9},{9,10},{10,1... | collective-permute-start | bytes 3686408 | tf_op jit(solution)/shard_map/ppermute | solution.py:17
  27.4 29.0 %collective-permute-start = (f32[2,4,15,2560]{3,1,0,2:T(4,128)}, f32[2,4,15,2560]{3,1,0,2:T(4,128)}, u32[]{:S(2)}, u32[]{:S(2)}) collective-permute-start(f32[2,4,15,2560]{3,1,0,2:T(4,128)} %get-tuple-element.66), channel_id=1, source_target_pairs={{1,0},{2,1},{3,2},{4,3},{5,4},{6,5},{7,6},{8,7},{9,8},{10,9},{11,1... | collective-permute-start | bytes 3686408 | tf_op jit(solution)/shard_map/ppermute | solution.py:17
  74.5 2.9 %copy-start = (f32[4,2,40,2560]{3,2,1,0:T(8,128)S(1)}, f32[4,2,40,2560]{3,2,1,0:T(8,128)}, u32[]{:S(2)}) copy-start(f32[4,2,40,2560]{3,2,1,0:T(8,128)} %gather_fusion.3) | copy-start | bytes 9830404
where the time goes:
time: 84 us; the launch traced here: 83.5 us
  local copies, waits for them, and re-layouts  26 us (31%)
  other arithmetic  22.8 us (27%)
  waiting for transfers between devices  20.5 us (24%)
  starting transfers between devices  10.1 us (12%)
  matrix products  2.61 us (3%)
  between operations  1.54 us (2%)
    ppermute x4, waiting for transfers between devices, from_behind(): return lax.ppermute(block, axis, route)  20.5 us
    ppermute x4, starting transfers between devices, from_behind(): return lax.ppermute(block, axis, route)  10.1 us
    gather x3, local copies, waits for them, and re-layouts, gather_lines(): chosen_indices = jnp.take(sweep_content, bounded_indices, axis=2)  7.14 us
    mul x2, other arithmetic, weighted(): return raw_lines.astype(jnp.float32) * weights.astype(jnp.float32)[:, None]  6.21 us
    unnamed x7, local copies, waits for them, and re-layouts  6.1 us
    reduce_sum x2, other arithmetic, looked(): aggregate = jnp.sum(shaped, axis=-2)  3.3 us
    dot_general x2, matrix products, looked(): return jnp.dot(aggregate, column_box, precision=lax.Precision.HIGHEST)  2.61 us
    select_n x1, other arithmetic, per_device(): second_image = jnp.take(combined_grid, image_couples[:, 1], axis=1)  2.49 us
  transfers between devices with their start and end apart: 4, of which 1 were waited for; matrix products, arithmetic and copies ran while one was open for 27% of the time, Pallas kernels for 0%

commit v1 on v0

v1 whole, which is shorter than its diff:
```python
import functools

import jax
import jax.numpy as jnp
from jax import lax
from jax.experimental import pallas as pl
from jax.experimental.pallas import tpu as pltpu
from jax.sharding import PartitionSpec as P

BLOCK_HEIGHT = 40
LOOK_ROWS = 5
LOOK_COLS = 20
MARGIN = 15
SLOT = 16
LANES = 128
CHUNKS = 4
MESH = pl.DeviceIdType.MESH
NT = (((1,), (1,)), ((), ()))


def row_of(index, boxes):
    return (index % boxes) * LOOK_ROWS + index // boxes


def kernel(
    n, start_ref, lines_ref, samples_ref, couples_ref, curve_ref, stack_ref,
    inter_ref, coher_ref,
    lines, sent, received, own, merged, looks, column_box, power, weight_out, weight_in,
    read_sem, send_sem, recv_sem, weight_send_sem, weight_recv_sem,
):
    me = lax.axis_index("az")
    parts, images, _, height, width = lines.shape
    pairs = couples_ref.shape[1]
    rows = BLOCK_HEIGHT
    boxes = rows // LOOK_ROWS
    step = width // CHUNKS
    has_down, has_up = me > 0, me < n - 1

    def columns(chunk):
        return pl.ds(chunk * step, step)

    def read(chunk):
        return pltpu.make_async_copy(
            stack_ref.at[:, :, :, :, columns(chunk)],
            lines.at[:, :, :, :, columns(chunk)],
            read_sem.at[chunk],
        )

    for chunk in range(CHUNKS):
        read(chunk).start()

    sides = ((0, has_down, me - 1, has_up), (1, has_up, me + 1, has_down))

    barrier = pltpu.get_barrier_semaphore()
    for side, has_target, target, _ in sides:
        @pl.when(has_target)
        def _():
            pl.semaphore_signal(
                barrier, inc=1, device_id={"az": target}, device_id_type=MESH
            )

    shift = start_ref[0] - me * rows
    slot_index = lax.broadcasted_iota(jnp.int32, (LANES, height), 0)
    line_index = lax.broadcasted_iota(jnp.int32, (LANES, height), 1)
    slot_row = jnp.where(
        slot_index < SLOT,
        jnp.where(slot_index < MARGIN, slot_index - MARGIN, -1000000),
        jnp.where(slot_index < SLOT + MARGIN, slot_index - SLOT + rows, -1000000),
    )
    select = jnp.where(line_index + shift == slot_row, 1.0, 0.0)
    out_index = lax.broadcasted_iota(jnp.int32, (rows, height), 0)
    out_line = lax.broadcasted_iota(jnp.int32, (rows, height), 1)
    curve_line = lax.broadcasted_iota(jnp.int32, (8, height), 1)
    curve = jnp.where(
        (curve_line >= lines_ref[0, 0]) & (curve_line < lines_ref[0, 1]),
        jnp.broadcast_to(curve_ref[...].astype(jnp.float32), (8, height)),
        0.0,
    )
    own_weights = jnp.where(
        out_line + shift == row_of(out_index, boxes),
        jnp.broadcast_to(curve[:1], (rows, height)),
        0.0,
    )
    own_total = jnp.sum(own_weights, axis=1, keepdims=True)
    operator = jnp.concatenate([select[: 2 * SLOT], own_weights], axis=0).astype(jnp.bfloat16)
    weight_out[...] = lax.dot_general(
        curve.astype(jnp.bfloat16), select.astype(jnp.bfloat16), NT,
        preferred_element_type=jnp.float32,
    )

    pl.semaphore_wait(barrier, has_down.astype(jnp.int32) + has_up.astype(jnp.int32))

    def weight_copy(side, target):
        return pltpu.make_async_remote_copy(
            src_ref=weight_out, dst_ref=weight_in.at[side],
            send_sem=weight_send_sem.at[side], recv_sem=weight_recv_sem.at[side],
            device_id={"az": target}, device_id_type=MESH,
        )

    def line_copy(side, chunk, target):
        span = pl.ds(side * SLOT, SLOT)
        return pltpu.make_async_remote_copy(
            src_ref=sent.at[:, span, columns(chunk)],
            dst_ref=received.at[:, span, columns(chunk)],
            send_sem=send_sem.at[side, chunk], recv_sem=recv_sem.at[side, chunk],
            device_id={"az": target}, device_id_type=MESH,
        )

    for side, has_target, target, _ in sides:
        @pl.when(has_target)
        def _():
            weight_copy(side, target).start()

    for chunk in range(CHUNKS):
        read(chunk).wait()
        sample = lax.broadcasted_iota(jnp.int32, (height, step), 1) + chunk * step
        keep = jnp.where(
            (sample >= samples_ref[0, 0]) & (sample < samples_ref[0, 1]), 1.0, 0.0
        ).astype(jnp.bfloat16)
        for c in range(parts):
            for a in range(images):
                image = c * images + a
                placed = jnp.dot(
                    operator, lines[c, a, 0, :, columns(chunk)] * keep,
                    preferred_element_type=jnp.float32,
                )
                sent[image, :, columns(chunk)] = placed[: 2 * SLOT].astype(jnp.bfloat16)
                own[image, :, columns(chunk)] = placed[2 * SLOT :]
        for side, has_target, target, _ in sides:
            @pl.when(has_target)
            def _():
                line_copy(side, chunk, target).start()

    for chunk in range(CHUNKS):
        sample = lax.broadcasted_iota(jnp.int32, (step, LANES), 0) + chunk * step
        low = lax.broadcasted_iota(jnp.int32, (step, LANES), 1) * LOOK_COLS
        column_box[chunk] = jnp.where(
            (sample >= low) & (sample < low + LOOK_COLS), 1.0, 0.0
        ).astype(jnp.bfloat16)

    for side, _, _, has_source in sides:
        @pl.when(jnp.logical_not(has_source))
        def _():
            weight_in[side] = jnp.zeros_like(weight_in[side])
            span = pl.ds(side * SLOT, SLOT)
            received[:, span, :] = jnp.zeros_like(received[:, span, :])

        @pl.when(has_source)
        def _():
            weight_copy(side, me).wait_recv()

    lane = lax.broadcasted_iota(jnp.int32, (rows, LANES), 1)
    row = row_of(lax.broadcasted_iota(jnp.int32, (rows, LANES), 0), boxes)
    taken = jnp.where(
        lane < SLOT,
        jnp.broadcast_to(weight_in[0][:1], (rows, LANES)),
        jnp.broadcast_to(weight_in[1][:1], (rows, LANES)),
    )
    target_row = jnp.where(lane < SLOT, lane + rows - MARGIN, lane - SLOT)
    spill = jnp.where((target_row == row) & (lane < 2 * SLOT), taken, 0.0)
    scale = jnp.broadcast_to(
        1.0 / (own_total + jnp.sum(spill, axis=1, keepdims=True)), (rows, LANES)
    )
    spill = spill[:, : 2 * SLOT].astype(jnp.bfloat16)

    def box_rows(values):
        return jnp.sum(values.reshape(LOOK_ROWS, boxes, LANES), axis=0)

    first = [couples_ref[0, p] for p in range(pairs)]
    second = [couples_ref[1, p] for p in range(pairs)]
    total = jnp.zeros(((2 * pairs + images) * boxes, LANES), jnp.float32)
    for chunk in range(CHUNKS):
        for side, _, _, has_source in sides:
            @pl.when(has_source)
            def _():
                line_copy(side, chunk, me).wait_recv()
        for image in range(parts * images):
            arrived = jnp.dot(
                spill, received[image, :, columns(chunk)],
                preferred_element_type=jnp.float32,
            )
            for tile in range(step // LANES):
                span = pl.ds(chunk * step + tile * LANES, LANES)
                merged[image, tile] = (
                    own[image, :, span] + arrived[:, tile * LANES : (tile + 1) * LANES]
                ) * scale
        for tile in range(step // LANES):
            span = pl.ds(tile * LANES, LANES)
            for p in range(pairs):
                re1, im1 = merged[first[p], tile], merged[first[p] + images, tile]
                re2, im2 = merged[second[p], tile], merged[second[p] + images, tile]
                looks[p, :, span] = box_rows(re1 * re2 + im1 * im2)
                looks[pairs + p, :, span] = box_rows(im1 * re2 - re1 * im2)
            for a in range(images):
                re, im = merged[a, tile], merged[images + a, tile]
                looks[2 * pairs + a, :, span] = box_rows(re * re + im * im)
        values = looks[...].reshape(total.shape[0], step)
        high = values.astype(jnp.bfloat16)
        rest = (values - high.astype(jnp.float32)).astype(jnp.bfloat16)
        box = column_box[chunk]
        total += jnp.dot(high, box, preferred_element_type=jnp.float32)
        total += jnp.dot(rest, box, preferred_element_type=jnp.float32)

    total = total.reshape(2 * pairs + images, boxes, LANES)
    power[...] = total[2 * pairs :]
    for p in range(pairs):
        re, im = total[p], total[pairs + p]
        inter_ref[0, p] = re / (LOOK_ROWS * LOOK_COLS)
        inter_ref[1, p] = im / (LOOK_ROWS * LOOK_COLS)
        coher_ref[p] = (re * re + im * im) / jnp.maximum(
            power[first[p]] * power[second[p]], 1.0
        )

    for side, has_target, target, _ in sides:
        @pl.when(has_target)
        def _():
            weight_copy(side, target).wait_send()
            for chunk in range(CHUNKS):
                line_copy(side, chunk, target).wait_send()


def per_device(
    n,
    sweep_stack,
    blend_curve,
    sweep_start_index,
    usable_azimuth_extent,
    usable_column_extent,
    image_couples,
):
    parts, images, _, height, width = sweep_stack.shape
    pairs = image_couples.shape[0]
    boxes = BLOCK_HEIGHT // LOOK_ROWS
    step = width // CHUNKS
    smem = pl.BlockSpec(memory_space=pltpu.SMEM)
    vmem = pl.BlockSpec(memory_space=pltpu.VMEM)
    count = parts * images
    return pl.pallas_call(
        functools.partial(kernel, n),
        out_shape=(
            jax.ShapeDtypeStruct((2, pairs, boxes, LANES), jnp.float32),
            jax.ShapeDtypeStruct((pairs, boxes, LANES), jnp.float32),
        ),
        in_specs=[smem, smem, smem, smem, vmem, pl.BlockSpec(memory_space=pl.ANY)],
        out_specs=(vmem, vmem),
        scratch_shapes=[
            pltpu.VMEM(sweep_stack.shape, jnp.bfloat16),
            pltpu.VMEM((count, 2 * SLOT, width), jnp.bfloat16),
            pltpu.VMEM((count, 2 * SLOT, width), jnp.bfloat16),
            pltpu.VMEM((count, BLOCK_HEIGHT, width), jnp.float32),
            pltpu.VMEM((count, step // LANES, BLOCK_HEIGHT, LANES), jnp.float32),
            pltpu.VMEM((2 * pairs + images, boxes, step), jnp.float32),
            pltpu.VMEM((CHUNKS, step, LANES), jnp.bfloat16),
            pltpu.VMEM((images, boxes, LANES), jnp.float32),
            pltpu.VMEM((8, LANES), jnp.float32),
            pltpu.VMEM((2, 8, LANES), jnp.float32),
            pltpu.SemaphoreType.DMA((CHUNKS,)),
            pltpu.SemaphoreType.DMA((2, CHUNKS)),
            pltpu.SemaphoreType.DMA((2, CHUNKS)),
            pltpu.SemaphoreType.DMA((2,)),
            pltpu.SemaphoreType.DMA((2,)),
        ],
        compiler_params=pltpu.CompilerParams(collective_id=0, has_side_effects=True),
    )(
        sweep_start_index,
        usable_azimuth_extent,
        usable_column_extent,
        image_couples.T,
        blend_curve,
        sweep_stack,
    )


def solution(mesh):
    return jax.shard_map(
        functools.partial(per_device, mesh.shape["az"]),
        mesh=mesh,
        in_specs=(
            P(None, None, ("groups", "az"), None, None),
            P(("groups", "az"), None),
            P(("groups", "az")),
            P(("groups", "az"), None),
            P(("groups", "az"), None),
            P("groups", None),
        ),
        out_specs=(P(None, "groups", "az", None), P("groups", "az", None)),
        check_vma=False,
    )
```

time: 84 us -> 24.9 us (0.30)
  local copies, waits for them, and re-layouts: 26 us -> 2.7 us
  other arithmetic: 22.8 us -> 0 us
  Pallas kernels: 0 us -> 20.7 us
  waiting for transfers between devices: 20.5 us -> 0 us
  starting transfers between devices: 10.1 us -> 0 us
  matrix products: 2.61 us -> 0 us
    pallas_call x0 -> x1, Pallas kernels: none -> 20.7 us  [per_device(): pl.pallas_call(functools.partial(kernel, n), out_shape=(jax.ShapeDtypeStr...]
    ppermute x4 -> x0, waiting for transfers between devices: 20.5 us -> none  [from_behind(): return lax.ppermute(block, axis, route)]
    gather x7 -> x0, local copies, waits for them, and re-layouts: 13.1 us -> none  [the longest x3 7.14 us: gather_lines(): chosen_indices = jnp.take(sweep_content, bounded_indices, axis=2)]
    ppermute x4 -> x0, starting transfers between devices: 10.1 us -> none  [from_behind(): return lax.ppermute(block, axis, route)]
    mul x2 -> x0, other arithmetic: 6.21 us -> none  [weighted(): return raw_lines.astype(jnp.float32) * weights.astype(jnp.float32)[:, None]]
    reduce_sum x4 -> x0, other arithmetic: 3.66 us -> none  [the longest x2 3.3 us: looked(): aggregate = jnp.sum(shaped, axis=-2)]
    scatter-add x4 -> x0, other arithmetic: 3.54 us -> none  [the longest x1 1.69 us: per_device(): cross_term = cross_term.at[:, :, :extent_rows].add(from_below)]
    unnamed x7 -> x2, local copies, waits for them, and re-layouts: 6.1 us -> 2.7 us
  transfers between devices with their start and end apart: 4 -> 0, of which waited for: 1 -> 0; matrix products, arithmetic and copies ran while one was open for 27% -> 0% of each run, Pallas kernels for 0% -> 0%
where the time goes in v1:
time: 24.9 us; the launch traced here: 24.7 us
  Pallas kernels  20.7 us (83%)
  local copies, waits for them, and re-layouts  2.7 us (11%)
  between operations  1.28 us (5%)
    pallas_call x1, Pallas kernels, per_device(): pl.pallas_call(functools.partial(kernel, n), out_shape=(jax.ShapeDtypeStr...  20.7 us
    unnamed x2, local copies, waits for them, and re-layouts  2.7 us

profile of v1, /device:TPU:11, one launch (start us, length us, event | category | flops | bytes accessed | tf_op | source)
XLA Modules:
  0.0 24.7 jit_solution(13210925399156782318)
XLA Ops:
  1.3 20.7 %shard_map.77 = (f32[2,4,8,128]{3,2,1,0:T(8,128)}, f32[4,8,128]{2,1,0:T(8,128)}) custom-call(s32[1]{0:T(128)S(6)} %copy.10.start_ref, s32[1,2]{1,0:T(1,128)} %lines_ref.1, s32[1,2]{1,0:T(1,128)} %samples_ref.1, s32[2,4]{1,0:T(2,128)} %bitcast.1, bf16[1,80]{1,0:T(2,128)(2,1)} %curve_ref.1, bf16[2,4,1,80,2560]{4,3,2,1,0:T(8,128)(2,1)} %stack_ref.1), custom_call_target="tpu_custom_call" | custom-call | tf_op jit(solution)/shard_map/pallas_call | solution.py:238
  22.0 1.4 %copy.11 = f32[2,4,8,128]{3,2,1,0:T(8,128)} copy(f32[2,4,8,128]{3,2,1,0:T(8,128)} %get-tuple-element.4) | data formatting | bytes 65536
  23.3 1.3 %copy.12 = f32[4,8,128]{2,1,0:T(8,128)} copy(f32[4,8,128]{2,1,0:T(8,128)} %get-tuple-element.5) | data formatting | bytes 32768

commit v2 on v1

--- a/solution.py
+++ b/solution.py
@@ -13,7 +13,7 @@
 MARGIN = 15
 SLOT = 16
 LANES = 128
-CHUNKS = 4
+CHUNKS = 10
 MESH = pl.DeviceIdType.MESH
 NT = (((1,), (1,)), ((), ()))
 
@@ -25,8 +25,8 @@
 def kernel(
     n, start_ref, lines_ref, samples_ref, couples_ref, curve_ref, stack_ref,
     inter_ref, coher_ref,
-    lines, sent, received, own, merged, looks, column_box, power, weight_out, weight_in,
-    read_sem, send_sem, recv_sem, weight_send_sem, weight_recv_sem,
+    lines, sent, received, own, merged, looks, column_box, power, weight_out, weight_in, start,
+    start_sem, read_sem, send_sem, recv_sem, weight_send_sem, weight_recv_sem,
 ):
     me = lax.axis_index("az")
     parts, images, _, height, width = lines.shape
@@ -46,6 +46,8 @@
             read_sem.at[chunk],
         )
 
+    start_read = pltpu.make_async_copy(start_ref, start, start_sem.at[0])
+    start_read.start()
     for chunk in range(CHUNKS):
         read(chunk).start()
 
@@ -59,7 +61,8 @@
                 barrier, inc=1, device_id={"az": target}, device_id_type=MESH
             )
 
-    shift = start_ref[0] - me * rows
+    start_read.wait()
+    shift = start[0] - me * rows
     slot_index = lax.broadcasted_iota(jnp.int32, (LANES, height), 0)
     line_index = lax.broadcasted_iota(jnp.int32, (LANES, height), 1)
     slot_row = jnp.where(
@@ -234,14 +237,15 @@
     step = width // CHUNKS
     smem = pl.BlockSpec(memory_space=pltpu.SMEM)
     vmem = pl.BlockSpec(memory_space=pltpu.VMEM)
+    hbm = pl.BlockSpec(memory_space=pltpu.HBM)
     count = parts * images
     return pl.pallas_call(
         functools.partial(kernel, n),
         out_shape=(
-            jax.ShapeDtypeStruct((2, pairs, boxes, LANES), jnp.float32),
-            jax.ShapeDtypeStruct((pairs, boxes, LANES), jnp.float32),
+            pltpu.VMEM((2, pairs, boxes, LANES), jnp.float32),
+            pltpu.VMEM((pairs, boxes, LANES), jnp.float32),
         ),
-        in_specs=[smem, smem, smem, smem, vmem, pl.BlockSpec(memory_space=pl.ANY)],
+        in_specs=[hbm, smem, smem, smem, vmem, hbm],
         out_specs=(vmem, vmem),
         scratch_shapes=[
             pltpu.VMEM(sweep_stack.shape, jnp.bfloat16),
@@ -254,13 +258,17 @@
             pltpu.VMEM((images, boxes, LANES), jnp.float32),
             pltpu.VMEM((8, LANES), jnp.float32),
             pltpu.VMEM((2, 8, LANES), jnp.float32),
+            pltpu.SMEM((1,), jnp.int32),
+            pltpu.SemaphoreType.DMA((1,)),
             pltpu.SemaphoreType.DMA((CHUNKS,)),
             pltpu.SemaphoreType.DMA((2, CHUNKS)),
             pltpu.SemaphoreType.DMA((2, CHUNKS)),
             pltpu.SemaphoreType.DMA((2,)),
             pltpu.SemaphoreType.DMA((2,)),
         ],
-        compiler_params=pltpu.CompilerParams(collective_id=0, has_side_effects=True),
+        compiler_params=pltpu.CompilerParams(
+            collective_id=0, has_side_effects=True
+        ),
     )(
         sweep_start_index,
         usable_azimuth_extent,

time: 24.9 us -> 22.5 us (0.904)
  local copies, waits for them, and re-layouts: 2.7 us -> 1.22 us
  Pallas kernels: 20.7 us -> 19.9 us
    unnamed x2, local copies, waits for them, and re-layouts: 2.7 us -> 1.22 us
    pallas_call x1, Pallas kernels: 20.7 us -> 19.9 us  [per_device(): pl.pallas_call(functools.partial(kernel, n), out_shape=(pltpu.VMEM((2, pa...]
where the time goes in v2:
time: 22.5 us; the launch traced here: 22.4 us
  Pallas kernels  19.9 us (88%)
  between operations  1.28 us (6%)
  local copies, waits for them, and re-layouts  1.22 us (5%)
    pallas_call x1, Pallas kernels, per_device(): pl.pallas_call(functools.partial(kernel, n), out_shape=(pltpu.VMEM((2, pa...  19.9 us
    unnamed x2, local copies, waits for them, and re-layouts  1.22 us

profile of v2, /device:TPU:11, one launch (start us, length us, event | category | flops | bytes accessed | tf_op | source)
XLA Modules:
  0.0 22.4 jit_solution(12301082711919040305)
XLA Ops:
  1.3 19.9 %shard_map.77 = (f32[2,4,8,128]{3,2,1,0:T(8,128)S(1)}, f32[4,8,128]{2,1,0:T(8,128)S(1)}) custom-call(s32[1]{0:T(128)S(6)} %copy.12.start_ref, s32[1,2]{1,0:T(1,128)} %lines_ref.1, s32[1,2]{1,0:T(1,128)} %samples_ref.1, s32[2,4]{1,0:T(2,128)} %bitcast.1, bf16[1,80]{1,0:T(2,128)(2,1)} %curve_ref.1, bf16[2,4,1,80,2560]{4,3,2,1,0:T(8,128)(2,1)} %stack_ref.1), custom_call_target="tpu_custom_call" | custom-call | tf_op jit(solution)/shard_map/pallas_call | solution.py:242
  21.2 0.6 %copy.10 = f32[2,4,8,128]{3,2,1,0:T(8,128)} copy(f32[2,4,8,128]{3,2,1,0:T(8,128)S(1)} %get-tuple-element.2) | data formatting | bytes 65536
  21.8 0.6 %copy.11 = f32[4,8,128]{2,1,0:T(8,128)} copy(f32[4,8,128]{2,1,0:T(8,128)S(1)} %get-tuple-element.3) | data formatting | bytes 32768

commit v3 on v2

--- a/solution.py
+++ b/solution.py
@@ -25,8 +25,8 @@
 def kernel(
     n, start_ref, lines_ref, samples_ref, couples_ref, curve_ref, stack_ref,
     inter_ref, coher_ref,
-    lines, sent, received, own, merged, looks, column_box, power, weight_out, weight_in, start,
-    start_sem, read_sem, send_sem, recv_sem, weight_send_sem, weight_recv_sem,
+    lines, sent, received, sent_rest, received_rest, own, merged, looks, column_box, power, weight_out, weight_in, start,
+    start_sem, read_sem, send_sem, recv_sem, rest_send_sem, rest_recv_sem, weight_send_sem, weight_recv_sem,
 ):
     me = lax.axis_index("az")
     parts, images, _, height, width = lines.shape
@@ -86,6 +86,15 @@
     )
     own_total = jnp.sum(own_weights, axis=1, keepdims=True)
     operator = jnp.concatenate([select[: 2 * SLOT], own_weights], axis=0).astype(jnp.bfloat16)
+    half = SLOT // 2
+    last = parts * images - 1
+    slots = lax.broadcasted_iota(jnp.int32, (2 * SLOT, step), 0)
+    turned = jnp.concatenate(
+        [select[side * SLOT + MARGIN - half : side * SLOT + MARGIN] if part == 0 else
+         select[side * SLOT : side * SLOT + half] for side in (0, 1) for part in (0, 1)],
+        axis=0,
+    )
+    last_operator = jnp.concatenate([turned, own_weights], axis=0).astype(jnp.bfloat16)
     weight_out[...] = lax.dot_general(
         curve.astype(jnp.bfloat16), select.astype(jnp.bfloat16), NT,
         preferred_element_type=jnp.float32,
@@ -109,6 +118,15 @@
             device_id={"az": target}, device_id_type=MESH,
         )
 
+    def rest_copy(side, chunk, target):
+        span = pl.ds(side * SLOT, SLOT)
+        part = pl.ds(chunk * step // 2, step // 2)
+        return pltpu.make_async_remote_copy(
+            src_ref=sent_rest.at[span, part], dst_ref=received_rest.at[span, part],
+            send_sem=rest_send_sem.at[side, chunk], recv_sem=rest_recv_sem.at[side, chunk],
+            device_id={"az": target}, device_id_type=MESH,
+        )
+
     for side, has_target, target, _ in sides:
         @pl.when(has_target)
         def _():
@@ -120,19 +138,33 @@
         keep = jnp.where(
             (sample >= samples_ref[0, 0]) & (sample < samples_ref[0, 1]), 1.0, 0.0
         ).astype(jnp.bfloat16)
-        for c in range(parts):
-            for a in range(images):
-                image = c * images + a
-                placed = jnp.dot(
-                    operator, lines[c, a, 0, :, columns(chunk)] * keep,
-                    preferred_element_type=jnp.float32,
-                )
-                sent[image, :, columns(chunk)] = placed[: 2 * SLOT].astype(jnp.bfloat16)
-                own[image, :, columns(chunk)] = placed[2 * SLOT :]
+        for image in range(last, -1, -1):
+            placed = jnp.dot(
+                last_operator if image == last else operator,
+                lines[image // images, image % images, 0, :, columns(chunk)] * keep,
+                preferred_element_type=jnp.float32,
+            )
+            own[image, :, columns(chunk)] = placed[2 * SLOT :]
+            if image == last:
+                extra = placed[: 2 * SLOT]
+                sent_rest[:, pl.ds(chunk * step // 2, step // 2)] = jnp.concatenate(
+                    [extra[side * SLOT : side * SLOT + half, part * step // 2 : (part + 1) * step // 2]
+                     for side in (0, 1) for part in (0, 1)], axis=0,
+                ).astype(jnp.bfloat16)
+            else:
+                fill = placed[: 2 * SLOT]
+                for side in (0, 1):
+                    at = side * SLOT + half + image
+                    fill = jnp.where(
+                        slots == side * SLOT + MARGIN,
+                        jnp.broadcast_to(extra[at : at + 1], (2 * SLOT, step)), fill,
+                    )
+                sent[image, :, columns(chunk)] = fill.astype(jnp.bfloat16)
         for side, has_target, target, _ in sides:
             @pl.when(has_target)
             def _():
                 line_copy(side, chunk, target).start()
+                rest_copy(side, chunk, target).start()
 
     for chunk in range(CHUNKS):
         sample = lax.broadcasted_iota(jnp.int32, (step, LANES), 0) + chunk * step
@@ -147,6 +179,7 @@
             weight_in[side] = jnp.zeros_like(weight_in[side])
             span = pl.ds(side * SLOT, SLOT)
             received[:, span, :] = jnp.zeros_like(received[:, span, :])
+            received_rest[span, :] = jnp.zeros_like(received_rest[span, :])
 
         @pl.when(has_source)
         def _():
@@ -165,6 +198,26 @@
         1.0 / (own_total + jnp.sum(spill, axis=1, keepdims=True)), (rows, LANES)
     )
     spill = spill[:, : 2 * SLOT].astype(jnp.bfloat16)
+
+    slot_from = lax.broadcasted_iota(jnp.int32, (2 * SLOT, 2 * SLOT), 0)
+    slot_to = lax.broadcasted_iota(jnp.int32, (2 * SLOT, 2 * SLOT), 1)
+
+    def moved(match):
+        order = jnp.where(match, 1.0, 0.0).astype(jnp.bfloat16)
+        return jnp.dot(spill, order, preferred_element_type=jnp.float32).astype(jnp.bfloat16)
+
+    spills = [
+        jnp.concatenate(
+            [spill, moved((slot_to % SLOT == MARGIN) & (slot_from == slot_to - MARGIN + image))],
+            axis=0,
+        )
+        for image in range(last)
+    ]
+    rest_spills = [
+        moved((slot_to % SLOT // half == part)
+              & (slot_from == slot_to - part * half + MARGIN - half))
+        for part in (0, 1)
+    ]
 
     def box_rows(values):
         return jnp.sum(values.reshape(LOOK_ROWS, boxes, LANES), axis=0)
@@ -177,15 +230,25 @@
             @pl.when(has_source)
             def _():
                 line_copy(side, chunk, me).wait_recv()
-        for image in range(parts * images):
-            arrived = jnp.dot(
-                spill, received[image, :, columns(chunk)],
-                preferred_element_type=jnp.float32,
-            )
+                rest_copy(side, chunk, me).wait_recv()
+        rest = received_rest[:, pl.ds(chunk * step // 2, step // 2)]
+        tail = jnp.concatenate(
+            [jnp.dot(matrix, rest, preferred_element_type=jnp.float32) for matrix in rest_spills],
+            axis=1,
+        )
+        for image in range(last + 1):
+            if image < last:
+                arrived = jnp.dot(
+                    spills[image], received[image, :, columns(chunk)],
+                    preferred_element_type=jnp.float32,
+                )
+                tail += arrived[rows:]
+            else:
+                arrived = tail
             for tile in range(step // LANES):
                 span = pl.ds(chunk * step + tile * LANES, LANES)
                 merged[image, tile] = (
-                    own[image, :, span] + arrived[:, tile * LANES : (tile + 1) * LANES]
+                    own[image, :, span] + arrived[:rows, tile * LANES : (tile + 1) * LANES]
                 ) * scale
         for tile in range(step // LANES):
             span = pl.ds(tile * LANES, LANES)
@@ -220,6 +283,7 @@
             weight_copy(side, target).wait_send()
             for chunk in range(CHUNKS):
                 line_copy(side, chunk, target).wait_send()
+                rest_copy(side, chunk, target).wait_send()
 
 
 def per_device(
@@ -249,8 +313,10 @@
         out_specs=(vmem, vmem),
         scratch_shapes=[
             pltpu.VMEM(sweep_stack.shape, jnp.bfloat16),
-            pltpu.VMEM((count, 2 * SLOT, width), jnp.bfloat16),
-            pltpu.VMEM((count, 2 * SLOT, width), jnp.bfloat16),
+            pltpu.VMEM((count - 1, 2 * SLOT, width), jnp.bfloat16),
+            pltpu.VMEM((count - 1, 2 * SLOT, width), jnp.bfloat16),
+            pltpu.VMEM((2 * SLOT, width // 2), jnp.bfloat16),
+            pltpu.VMEM((2 * SLOT, width // 2), jnp.bfloat16),
             pltpu.VMEM((count, BLOCK_HEIGHT, width), jnp.float32),
             pltpu.VMEM((count, step // LANES, BLOCK_HEIGHT, LANES), jnp.float32),
             pltpu.VMEM((2 * pairs + images, boxes, step), jnp.float32),
@@ -261,6 +327,8 @@
             pltpu.SMEM((1,), jnp.int32),
             pltpu.SemaphoreType.DMA((1,)),
             pltpu.SemaphoreType.DMA((CHUNKS,)),
+            pltpu.SemaphoreType.DMA((2, CHUNKS)),
+            pltpu.SemaphoreType.DMA((2, CHUNKS)),
             pltpu.SemaphoreType.DMA((2, CHUNKS)),
             pltpu.SemaphoreType.DMA((2, CHUNKS)),
             pltpu.SemaphoreType.DMA((2,)),

time: 22.5 us -> 22.2 us (0.987)
  Pallas kernels: 19.9 us -> 19.6 us
    pallas_call x1, Pallas kernels: 19.9 us -> 19.6 us  [per_device(): pl.pallas_call(functools.partial(kernel, n), out_shape=(pltpu.VMEM((2, pa...]
where the time goes in v3:
time: 22.2 us; the launch traced here: 22.1 us
  Pallas kernels  19.6 us (88%)
  between operations  1.28 us (6%)
  local copies, waits for them, and re-layouts  1.22 us (5%)
    pallas_call x1, Pallas kernels, per_device(): pl.pallas_call(functools.partial(kernel, n), out_shape=(pltpu.VMEM((2, pa...  19.6 us
    unnamed x2, local copies, waits for them, and re-layouts  1.22 us

profile of v3, /device:TPU:11, one launch (start us, length us, event | category | flops | bytes accessed | tf_op | source)
XLA Modules:
  0.0 22.1 jit_solution(15629860442596737504)
XLA Ops:
  1.3 19.6 %shard_map.77 = (f32[2,4,8,128]{3,2,1,0:T(8,128)S(1)}, f32[4,8,128]{2,1,0:T(8,128)S(1)}) custom-call(s32[1]{0:T(128)S(6)} %copy.12.start_ref, s32[1,2]{1,0:T(1,128)} %lines_ref.1, s32[1,2]{1,0:T(1,128)} %samples_ref.1, s32[2,4]{1,0:T(2,128)} %bitcast.1, bf16[1,80]{1,0:T(2,128)(2,1)} %curve_ref.1, bf16[2,4,1,80,2560]{4,3,2,1,0:T(8,128)(2,1)} %stack_ref.1), custom_call_target="tpu_custom_call" | custom-call | tf_op jit(solution)/shard_map/pallas_call | solution.py:306
  20.8 0.6 %copy.10 = f32[2,4,8,128]{3,2,1,0:T(8,128)} copy(f32[2,4,8,128]{3,2,1,0:T(8,128)S(1)} %get-tuple-element.2) | data formatting | bytes 65536
  21.5 0.6 %copy.11 = f32[4,8,128]{2,1,0:T(8,128)} copy(f32[4,8,128]{2,1,0:T(8,128)S(1)} %get-tuple-element.3) | data formatting | bytes 32768
